TPU v7x, 32 devices: a whole 2x2x4 slice. The times are simulated.
32 devices in a mesh: dp: 16 (over z, y, core), tensor: 2 (over x).
Axes of the slice: x: 2, y: 2, z: 4, core: 2. Of those that a mesh axis runs over, the one named last changes fastest.
Arguments:
- tokens: bfloat16 [64, 144, 1024], P('dp', 'tensor'), may hold values from -150 to 150
- cotangent: bfloat16 [64, 144, 1024], P('dp', 'tensor'), may hold values from -6 to 6
- dispatch_weight: bfloat16 [1024, 32], replicated, may hold values from -3 to 3
- w_in: bfloat16 [32, 1024, 4096], P('dp', None, 'tensor'), may hold values from -0.1875 to 0.1875
- w_out: bfloat16 [32, 4096, 1024], P('dp', 'tensor'), may hold values from -0.09375 to 0.09375
Outputs:
- grad_tokens: bfloat16 [64, 144, 1024], P('dp', 'tensor')
- grad_router: float32 [1024, 32], replicated
- grad_w_in: bfloat16 [32, 1024, 4096], P('dp', None, 'tensor')
- grad_w_out: bfloat16 [32, 4096, 1024], P('dp', 'tensor')
All inputs are finite; a program needn't handle non-finite values.
Results may differ from a plain program's by a relative error of at most 0.0079.
Values may be sent and summed in bfloat16 or wider, within the bound.
A program may use at most 64 MiB of HBM per device.

v0:
```python
import jax
import jax.numpy as jnp
from jax import lax
from jax.sharding import PartitionSpec as P


def to_experts(partial_rows):
    shared_part = lax.psum_scatter(partial_rows, "tensor", scatter_dimension=2, tiled=True).astype(
        jnp.bfloat16
    )
    arrived = lax.all_to_all(shared_part, "dp", split_axis=1, concat_axis=0, tiled=True)
    result = lax.all_gather(arrived, "tensor", axis=2, tiled=True)
    return result


def to_images(partial_rows):
    shared_part = lax.psum_scatter(partial_rows, "tensor", scatter_dimension=2, tiled=True).astype(
        jnp.bfloat16
    )
    arrived = lax.all_to_all(shared_part, "dp", split_axis=0, concat_axis=1, tiled=True)
    result = lax.all_gather(arrived, "tensor", axis=2, tiled=True)
    return result


def dispatch_softmax(logits):
    local_max = jnp.max(logits, axis=1)
    global_max = lax.pmax(local_max, "tensor")
    exponent = jnp.exp(logits - global_max[:, None, :])
    totals = lax.psum(jnp.sum(exponent, axis=1), "tensor")
    return exponent / totals[:, None, :]


def on_device(tokens, cotangent, dispatch_weight, w_in, w_out):
    wide = jnp.float32
    logits = jnp.einsum("isd,de->ise", tokens, dispatch_weight, preferred_element_type=wide)
    dispatch = dispatch_softmax(logits)
    combine = jax.nn.softmax(logits, axis=2)
    dispatch_low = dispatch.astype(jnp.bfloat16)
    combine_low = combine.astype(jnp.bfloat16)
    slot_inputs = to_experts(
        jnp.einsum("ise,isd->ied", dispatch_low, tokens, preferred_element_type=wide)
    )
    pre_act = jnp.einsum("ied,edf->ief", slot_inputs, w_in, preferred_element_type=wide)
    hidden_act, gelu_back = jax.vjp(jax.nn.gelu, pre_act)
    hidden_low = hidden_act.astype(jnp.bfloat16)
    slot_outputs = to_images(
        jnp.einsum("ief,efd->ied", hidden_low, w_out, preferred_element_type=wide)
    )
    grad_combine = jnp.einsum("isd,ied->ise", cotangent, slot_outputs, preferred_element_type=wide)
    grad_slots_out = to_experts(
        jnp.einsum("ise,isd->ied", combine_low, cotangent, preferred_element_type=wide)
    )
    grad_hidden = jnp.einsum("ied,efd->ief", grad_slots_out, w_out, preferred_element_type=wide)
    grad_pre = gelu_back(grad_hidden)[0].astype(jnp.bfloat16)
    grad_w_out = jnp.einsum(
        "ief,ied->efd", hidden_low, grad_slots_out, preferred_element_type=wide
    ).astype(jnp.bfloat16)
    grad_w_in = jnp.einsum(
        "ied,ief->edf", slot_inputs, grad_pre, preferred_element_type=wide
    ).astype(jnp.bfloat16)
    grad_slots_in = to_images(
        jnp.einsum("ief,edf->ied", grad_pre, w_in, preferred_element_type=wide)
    )
    grad_dispatch = jnp.einsum("isd,ied->ise", tokens, grad_slots_in, preferred_element_type=wide)
    column_dot = lax.psum(jnp.sum(grad_dispatch * dispatch, axis=1), "tensor")
    row_dot = jnp.sum(grad_combine * combine, axis=2, keepdims=True)
    grad_logits = (
        combine * (grad_combine - row_dot) + dispatch * (grad_dispatch - column_dot[:, None, :])
    ).astype(jnp.bfloat16)
    token_part = jnp.einsum(
        "ise,ied->isd", dispatch_low, grad_slots_in, preferred_element_type=wide
    )
    router_part = jnp.einsum(
        "ise,de->isd", grad_logits, dispatch_weight, preferred_element_type=wide
    )
    grad_tokens = (token_part + router_part).astype(jnp.bfloat16)
    local_router = jnp.einsum("isd,ise->de", tokens, grad_logits, preferred_element_type=wide)
    grad_router = lax.psum(local_router, ("dp", "tensor"))
    return (grad_tokens, grad_router, grad_w_in, grad_w_out)


def solution(mesh):
    return jax.shard_map(
        on_device,
        mesh=mesh,
        in_specs=(
            P("dp", "tensor", None),
            P("dp", "tensor", None),
            P(),
            P("dp", None, "tensor"),
            P("dp", "tensor", None),
        ),
        out_specs=(P("dp", "tensor", None), P(), P("dp", None, "tensor"), P("dp", "tensor", None)),
        check_vma=False,
    )
```

profile of v0, /device:TPU:0, one launch (start us, length us, event | category | flops | bytes accessed | tf_op | source)
XLA Modules:
  0.0 270.4 jit_solution(4491643558524088509)
XLA Ops:
  7.2 1.0 copy-done
  8.2 1.3 fusion.37
  9.5 0.2 fusion.38
  9.7 2.1 fusion.26
  11.8 0.0 reduce-scatter.7.cloned.1.call-start
  11.9 5.9 %pmax.7 = f32[4,32]{1,0:T(4,128)S(1)} all-reduce(f32[4,32]{1,0:T(4,128)S(1)} %get-tuple-element.4), channel_id=1, replica_groups=mesh['dp'=16,'tensor'=2] {'tensor'}, use_global_device_ids=true, to_apply=%region_1.0 | all-reduce | flops 128 | bytes 1024 | tf_op jit(solution)/shard_map/pmax | solution.py:27
  17.7 0.2 fusion.25
  17.9 4.9 %psum.21 = f32[4,32]{1,0:T(4,128)S(1)} all-reduce(f32[4,32]{1,0:T(4,128)S(1)} %fusion.25), channel_id=1, replica_groups=mesh['dp'=16,'tensor'=2] {'tensor'}, use_global_device_ids=true, to_apply=%region_3.0 | all-reduce | flops 128 | bytes 1024 | tf_op jit(solution)/shard_map/psum | solution.py:29
  22.9 1.1 fusion.29
  24.0 5.4 %reduce-scatter.5.cloned.1.call-done = f32[4,32,512]{2,1,0:T(8,128)} async-done(((f32[4,32,1024]{2,1,0:T(8,128)}), f32[4,32,512]{2,1,0:T(8,128)}) %reduce-scatter.5.cloned.1.call-update) | async-done | bytes 262160 | tf_op jit(solution)/shard_map/reduce_scatter | solution.py:8
  29.4 1.0 convert_element_type.38
  30.3 0.8 copy.13
  31.1 5.6 %all-to-all-start = ((bf16[4,32,512]{2,0,1:T(4,128)(2,1)}), bf16[4,32,512]{2,0,1:T(4,128)(2,1)S(1)}, u32[]{:S(2)}, u32[]{:S(2)}) async-start(bf16[4,32,512]{2,0,1:T(4,128)(2,1)} %copy.13), calls=%async_computation.1 | async-start | bytes 262144 | tf_op jit(solution)/shard_map/all_to_all | solution.py:11
  36.7 10.1 %reduce-scatter.7.cloned.1.call-done = f32[4,32,512]{2,1,0:T(8,128)} async-done(((f32[4,32,1024]{2,1,0:T(8,128)}), f32[4,32,512]{2,1,0:T(8,128)}) %reduce-scatter.7.cloned.1.call-update) | async-done | bytes 262160 | tf_op jit(solution)/shard_map/reduce_scatter | solution.py:8
  46.9 1.0 convert_element_type.39
  47.8 0.8 copy.15
  48.6 5.6 %all-to-all-start.1 = ((bf16[4,32,512]{2,0,1:T(4,128)(2,1)}), bf16[4,32,512]{2,0,1:T(4,128)(2,1)S(1)}, u32[]{:S(2)}, u32[]{:S(2)}) async-start(bf16[4,32,512]{2,0,1:T(4,128)(2,1)} %copy.15), calls=%async_computation.3 | async-start | bytes 262144 | tf_op jit(solution)/shard_map/all_to_all | solution.py:11
  54.4 6.5 %all_gather.12 = bf16[64,2,1024]{2,0,1:T(8,128)(2,1)S(1)} all-gather(bf16[64,2,512]{2,0,1:T(8,128)(2,1)S(1)} %all_to_all.55), channel_id=1, replica_groups=mesh['dp'=16,'tensor'=2] {'tensor'}, dimensions={2}, use_global_device_ids=true | all-gather | bytes 393216 | tf_op jit(solution)/shard_map/all_gather | solution.py:12
  60.8 1.3 all-to-all-done.1
  62.2 5.8 %all_gather.13 = bf16[64,2,1024]{2,0,1:T(8,128)(2,1)S(1)} all-gather(bf16[64,2,512]{2,0,1:T(8,128)(2,1)S(1)} %all_to_all.59), channel_id=1, replica_groups=mesh['dp'=16,'tensor'=2] {'tensor'}, dimensions={2}, use_global_device_ids=true | all-gather | bytes 393216 | tf_op jit(solution)/shard_map/all_gather | solution.py:12
  68.0 5.1 %convolution_bitcast_fusion = f32[64,2,2048]{2,0,1:T(8,128)S(1)} fusion(bf16[64,2,1024]{2,0,1:T(8,128)(2,1)S(1)} %all_gather.13, bf16[2,1024,2048]{2,1,0:T(8,128)(2,1)} %param.8), kind=kOutput, calls=%fused_computation.4 | convolution fusion | flops 536870912 | bytes 9699328 | tf_op jit(solution)/shard_map/ied,edf->ief/dot_general | solution.py:43
  73.1 2.9 %fusion.16 = bf16[64,2,2048]{2,0,1:T(8,128)(2,1)S(1)} fusion(f32[64,2,2048]{2,0,1:T(8,128)S(1)} %convolution_bitcast_fusion, bf16[64,2,1024]{2,0,1:T(8,128)(2,1)S(1)} %all_gather.12, bf16[2,2048,1024]{2,1,0:T(8,128)(2,1)S(1)} %copy-done.1), kind=kOutput, calls=%fused_computation.28 | convolution fusion | flops 542113792 | bytes 10223616 | tf_op jit(solution)/shard_map/ied,efd->ief/dot_general | solution.py:53
  76.0 3.5 %convolution_bitcast_fusion.3 = f32[64,2,1024]{2,0,1:T(8,128)} fusion(bf16[64,2,2048]{2,0,1:T(8,128)(2,1)S(1)} %fusion.16, bf16[2,1024,2048]{2,1,0:T(8,128)(2,1)S(1)} %bitcast.67), kind=kOutput, calls=%fused_computation.11 | convolution fusion | flops 536870912 | bytes 9437184 | tf_op jit(solution)/shard_map/ief,edf->ied/dot_general | solution.py:62
  79.6 5.7 %convolution_bitcast_fusion.2 = f32[64,2,1024]{2,0,1:T(8,128)} fusion(bf16[2,2048,1024]{2,1,0:T(8,128)(2,1)} %param.9, f32[64,2,2048]{2,0,1:T(8,128)S(1)} %convolution_bitcast_fusion), kind=kOutput, calls=%fused_computation.10 | convolution fusion | flops 539230208 | bytes 9961472 | tf_op jit(solution)/shard_map/ief,efd->ied/dot_general | solution.py:47
  85.3 5.8 %convolution_convert_fusion = bf16[2,2048,1024]{2,1,0:T(8,128)(2,1)} fusion(bf16[64,2,1024]{2,0,1:T(8,128)(2,1)S(1)} %all_gather.12, f32[64,2,2048]{2,0,1:T(8,128)S(1)} %convolution_bitcast_fusion), kind=kOutput, calls=%fused_computation.2 | convolution fusion | flops 543424512 | bytes 9699328 | tf_op jit(solution)/shard_map/ief,ied->efd/dot_general | solution.py:55
  91.1 2.0 reduce-scatter.9.cloned.1.call-done
  93.1 1.0 convert_element_type.41
  94.1 0.8 copy.17
  94.9 5.6 %all-to-all-start.2 = ((bf16[64,2,512]{2,1,0:T(2,128)(2,1)}), bf16[64,2,512]{2,1,0:T(2,128)(2,1)S(1)}, u32[]{:S(2)}, u32[]{:S(2)}) async-start(bf16[64,2,512]{2,1,0:T(2,128)(2,1)} %copy.17), calls=%async_computation.5 | async-start | bytes 262144 | tf_op jit(solution)/shard_map/all_to_all | solution.py:20
  100.5 5.8 %convolution_convert_fusion.1 = bf16[2,1024,2048]{2,1,0:T(8,128)(2,1)} fusion(bf16[64,2,1024]{2,0,1:T(8,128)(2,1)S(1)} %all_gather.13, bf16[64,2,2048]{2,0,1:T(8,128)(2,1)S(1)} %fusion.16), kind=kOutput, calls=%fused_computation.3 | convolution fusion | flops 541065216 | bytes 9175040 | tf_op jit(solution)/shard_map/ied,ief->edf/dot_general | solution.py:58
  106.3 4.2 %reduce-scatter.11.cloned.1.call-done = f32[64,2,512]{2,0,1:T(8,128)} async-done(((f32[64,2,1024]{2,0,1:T(8,128)}), f32[64,2,512]{2,0,1:T(8,128)}) %reduce-scatter.11.cloned.1.call-update) | async-done | bytes 262160 | tf_op jit(solution)/shard_map/reduce_scatter | solution.py:17
  110.4 1.0 convert_element_type.43
  111.4 0.8 copy.19
  112.2 5.6 %all-to-all-start.3 = ((bf16[64,2,512]{2,1,0:T(2,128)(2,1)}), bf16[64,2,512]{2,1,0:T(2,128)(2,1)S(1)}, u32[]{:S(2)}, u32[]{:S(2)}) async-start(bf16[64,2,512]{2,1,0:T(2,128)(2,1)} %copy.19), calls=%async_computation.7 | async-start | bytes 262144 | tf_op jit(solution)/shard_map/all_to_all | solution.py:20
  117.9 0.1 copy.26
  118.0 0.1 all_to_all.63
  118.1 6.5 %all_gather.14 = bf16[4,32,1024]{2,1,0:T(8,128)(2,1)S(1)} all-gather(bf16[4,32,512]{2,1,0:T(8,128)(2,1)S(1)} %all_to_all.63), channel_id=1, replica_groups=mesh['dp'=16,'tensor'=2] {'tensor'}, dimensions={2}, use_global_device_ids=true | all-gather | bytes 393216 | tf_op jit(solution)/shard_map/all_gather | solution.py:21
  124.5 0.4 multiply_reduce_fusion.1
  124.9 4.9 %psum.22 = f32[4,32]{1,0:T(4,128)S(1)} all-reduce(f32[4,32]{1,0:T(4,128)S(1)} %get-tuple-element.8), channel_id=1, replica_groups=mesh['dp'=16,'tensor'=2] {'tensor'}, use_global_device_ids=true, to_apply=%region_12.0 | all-reduce | flops 128 | bytes 1024 | tf_op jit(solution)/shard_map/psum | solution.py:65
  129.9 0.1 copy.25
  129.9 0.1 all_to_all.67
  130.0 5.6 %all_gather.15 = bf16[4,32,1024]{2,1,0:T(8,128)(2,1)S(1)} all-gather(bf16[4,32,512]{2,1,0:T(8,128)(2,1)S(1)} %all_to_all.67), channel_id=1, replica_groups=mesh['dp'=16,'tensor'=2] {'tensor'}, dimensions={2}, use_global_device_ids=true | all-gather | bytes 393216 | tf_op jit(solution)/shard_map/all_gather | solution.py:21
  135.7 0.3 convolution_bitcast_fusion.6
  135.9 1.0 convolution_bitcast_fusion.4
  137.0 0.4 fusion.9
  137.5 1.3 fusion.2
  138.7 123.5 %all-reduce.2.cloned.1.call-done = f32[1024,32]{0,1:T(8,128)} async-done(((f32[1024,32]{0,1:T(8,128)}), f32[1024,32]{0,1:T(8,128)}) %all-reduce.2.cloned.1.call-update) | async-done | bytes 131088 | tf_op jit(solution)/shard_map/psum | solution.py:78
  262.3 1.6 copy.30
  (28 shorter events, 0.5 us)
Async XLA Ops:
  7.2 1.1 copy-start
  7.2 22.2 %reduce-scatter.5.cloned.1.call-start = ((), (), s32[]{:S(2)}) async-start(), calls=%async_computation.8 | async-start | bytes 786432 | tf_op jit(solution)/shard_map/reduce_scatter | solution.py:8
  11.8 35.0 %reduce-scatter.7.cloned.1.call-start = ((), (), s32[]{:S(2)}) async-start(), calls=%async_computation.9 | async-start | bytes 786432 | tf_op jit(solution)/shard_map/reduce_scatter | solution.py:8
  31.1 17.5 %all-to-all-start = ((bf16[4,32,512]{2,0,1:T(4,128)(2,1)}), bf16[4,32,512]{2,0,1:T(4,128)(2,1)S(1)}, u32[]{:S(2)}, u32[]{:S(2)}) async-start(bf16[4,32,512]{2,0,1:T(4,128)(2,1)} %copy.13), calls=%async_computation.1 | async-start | bytes 262144 | tf_op jit(solution)/shard_map/all_to_all | solution.py:11
  48.6 13.5 %all-to-all-start.1 = ((bf16[4,32,512]{2,0,1:T(4,128)(2,1)}), bf16[4,32,512]{2,0,1:T(4,128)(2,1)S(1)}, u32[]{:S(2)}, u32[]{:S(2)}) async-start(bf16[4,32,512]{2,0,1:T(4,128)(2,1)} %copy.15), calls=%async_computation.3 | async-start | bytes 262144 | tf_op jit(solution)/shard_map/all_to_all | solution.py:11
  54.2 38.9 %reduce-scatter.9.cloned.1.call-start = ((), (), s32[]{:S(2)}) async-start(), calls=%async_computation.10 | async-start | bytes 786432 | tf_op jit(solution)/shard_map/reduce_scatter | solution.py:17
  62.2 10.9 %copy-start.1 = (bf16[2,2048,1024]{2,1,0:T(8,128)(2,1)S(1)}, bf16[2,2048,1024]{2,1,0:T(8,128)(2,1)}, u32[]{:S(2)}) copy-start(bf16[2,2048,1024]{2,1,0:T(8,128)(2,1)} %param.9) | copy-start | bytes 25165828
  62.2 13.8 %slice-start = ((s8[8388608]{0:T(1024)(128)(4,1)}), s8[4194304]{0:T(1024)(128)(4,1)S(1)}, s32[]{:S(2)}) async-start(s8[8388608]{0:T(1024)(128)(4,1)} %bitcast.66), calls=%async_computation.13 | async-start | bytes 8388608
  68.0 8.0 %slice-start.1 = ((s8[8388608]{0:T(1024)(128)(4,1)}), s8[4194304]{0:T(1024)(128)(4,1)S(1)}, s32[]{:S(2)}) async-start(s8[8388608]{0:T(1024)(128)(4,1)} %bitcast.66), calls=%async_computation.14 | async-start | bytes 8388608
  79.5 30.9 %reduce-scatter.11.cloned.1.call-start = ((), (), s32[]{:S(2)}) async-start(), calls=%async_computation.11 | async-start | bytes 786432 | tf_op jit(solution)/shard_map/reduce_scatter | solution.py:17
  91.1 44.6 %copy-start.2 = (bf16[4,72,1024]{2,1,0:T(8,128)(2,1)S(1)}, bf16[4,72,1024]{2,1,0:T(8,128)(2,1)}, u32[]{:S(2)}) copy-start(bf16[4,72,1024]{2,1,0:T(8,128)(2,1)} %param.6) | copy-start | bytes 1769476
  91.1 45.9 %copy-start.3 = (bf16[1024,32]{0,1:T(8,128)(2,1)S(1)}, bf16[1024,32]{0,1:T(8,128)(2,1)}, u32[]{:S(2)}) copy-start(bf16[1024,32]{0,1:T(8,128)(2,1)} %param.7) | copy-start | bytes 196612
  94.9 17.3 %all-to-all-start.2 = ((bf16[64,2,512]{2,1,0:T(2,128)(2,1)}), bf16[64,2,512]{2,1,0:T(2,128)(2,1)S(1)}, u32[]{:S(2)}, u32[]{:S(2)}) async-start(bf16[64,2,512]{2,1,0:T(2,128)(2,1)} %copy.17), calls=%async_computation.5 | async-start | bytes 262144 | tf_op jit(solution)/shard_map/all_to_all | solution.py:20
  112.2 17.6 %all-to-all-start.3 = ((bf16[64,2,512]{2,1,0:T(2,128)(2,1)}), bf16[64,2,512]{2,1,0:T(2,128)(2,1)S(1)}, u32[]{:S(2)}, u32[]{:S(2)}) async-start(bf16[64,2,512]{2,1,0:T(2,128)(2,1)} %copy.19), calls=%async_computation.7 | async-start | bytes 262144 | tf_op jit(solution)/shard_map/all_to_all | solution.py:20
  117.9 144.4 %all-reduce.2.cloned.1.call-start = ((), (), s32[]{:S(2)}) async-start(), calls=%async_computation.12 | async-start | bytes 262144 | tf_op jit(solution)/shard_map/psum | solution.py:78
Sparse Core Ops, SparseCore 0:
  11.9 17.3 reduce-scatter.4
  32.2 14.6 reduce-scatter.6
  79.6 13.4 reduce-scatter.8
  95.8 14.6 reduce-scatter.10
  137.6 124.6 all-reduce.1
where the time goes:
time: 271 us; the launch traced here: 270 us
  waiting for transfers between devices  147 us (54%)
  blocking collectives  40.1 us (15%)
  matrix products  36.6 us (14%)
  starting transfers between devices  22.7 us (8%)
  between operations  14 us (5%)
  local copies, waits for them, and re-layouts  6.18 us (2%)
  other arithmetic  4.2 us (2%)
    psum x1, waiting for transfers between devices, on_device(): grad_router = lax.psum(local_router, ('dp', 'tensor'))  124 us
    reduce_scatter x2, waiting for transfers between devices, to_experts(): lax.psum_scatter(partial_rows, 'tensor', scatter_dimension=2, tiled=True)  15.5 us
    all_gather x2, blocking collectives, to_experts(): result = lax.all_gather(arrived, 'tensor', axis=2, tiled=True)  12.2 us
    all_gather x2, blocking collectives, to_images(): result = lax.all_gather(arrived, 'tensor', axis=2, tiled=True)  12.1 us
    all_to_all x2, starting transfers between devices, to_images(): lax.all_to_all(shared_part, 'dp', split_axis=0, concat_axis=1, tiled=True)  11.3 us
    all_to_all x2, starting transfers between devices, to_experts(): lax.all_to_all(shared_part, 'dp', split_axis=1, concat_axis=0, tiled=True)  11.2 us
    reduce_scatter x2, waiting for transfers between devices, to_images(): lax.psum_scatter(partial_rows, 'tensor', scatter_dimension=2, tiled=True)  6.15 us
    pmax x1, blocking collectives, dispatch_softmax(): global_max = lax.pmax(local_max, 'tensor')  5.87 us
  transfers between devices with their start and end apart: 9, of which 6 were waited for; matrix products, arithmetic and copies ran while one was open for 10% of the time, Pallas kernels for 0%

commit v1 on v0

--- a/solution.py
+++ b/solution.py
@@ -75,7 +75,8 @@
     )
     grad_tokens = (token_part + router_part).astype(jnp.bfloat16)
     local_router = jnp.einsum("isd,ise->de", tokens, grad_logits, preferred_element_type=wide)
-    grad_router = lax.psum(local_router, ("dp", "tensor"))
+    arr_now = lax.psum(local_router, "tensor")
+    grad_router = lax.psum(arr_now, "dp")
     return (grad_tokens, grad_router, grad_w_in, grad_w_out)
 
 

time: 271 us -> 261 us (0.963)
  waiting for transfers between devices: 147 us -> 135 us
    psum x1 -> x2, waiting for transfers between devices: 124 us -> 112 us  [the longest x1 90.3 us: on_device(): grad_router = lax.psum(arr_now, 'dp')]
  transfers between devices with their start and end apart: 9 -> 10, of which waited for: 6 -> 7; matrix products, arithmetic and copies ran while one was open for 10% -> 11% of each run, Pallas kernels for 0% -> 0%
where the time goes in v1:
time: 261 us; the launch traced here: 259 us
  waiting for transfers between devices  135 us (52%)
  blocking collectives  40.1 us (15%)
  matrix products  36.6 us (14%)
  starting transfers between devices  22.8 us (9%)
  between operations  14.3 us (5%)
  local copies, waits for them, and re-layouts  6.18 us (2%)
  other arithmetic  4.2 us (2%)
    psum x1, waiting for transfers between devices, on_device(): grad_router = lax.psum(arr_now, 'dp')  90.3 us
    psum x1, waiting for transfers between devices, on_device(): arr_now = lax.psum(local_router, 'tensor')  21.3 us
    reduce_scatter x2, waiting for transfers between devices, to_experts(): lax.psum_scatter(partial_rows, 'tensor', scatter_dimension=2, tiled=True)  15.5 us
    all_gather x2, blocking collectives, to_experts(): result = lax.all_gather(arrived, 'tensor', axis=2, tiled=True)  12.2 us
    all_gather x2, blocking collectives, to_images(): result = lax.all_gather(arrived, 'tensor', axis=2, tiled=True)  12.1 us
    all_to_all x2, starting transfers between devices, to_images(): lax.all_to_all(shared_part, 'dp', split_axis=0, concat_axis=1, tiled=True)  11.3 us
    all_to_all x2, starting transfers between devices, to_experts(): lax.all_to_all(shared_part, 'dp', split_axis=1, concat_axis=0, tiled=True)  11.2 us
    reduce_scatter x2, waiting for transfers between devices, to_images(): lax.psum_scatter(partial_rows, 'tensor', scatter_dimension=2, tiled=True)  6.15 us
  transfers between devices with their start and end apart: 10, of which 7 were waited for; matrix products, arithmetic and copies ran while one was open for 11% of the time, Pallas kernels for 0%

profile of v1, /device:TPU:0, one launch (start us, length us, event | category | flops | bytes accessed | tf_op | source)
XLA Modules:
  0.0 258.8 jit_solution(4350163683142319825)
XLA Ops:
  7.2 1.0 copy-done
  8.2 1.3 fusion.37
  9.5 0.2 fusion.38
  9.7 2.1 fusion.26
  11.9 5.9 %pmax.7 = f32[4,32]{1,0:T(4,128)S(1)} all-reduce(f32[4,32]{1,0:T(4,128)S(1)} %get-tuple-element.4), channel_id=1, replica_groups=mesh['dp'=16,'tensor'=2] {'tensor'}, use_global_device_ids=true, to_apply=%region_1.0 | all-reduce | flops 128 | bytes 1024 | tf_op jit(solution)/shard_map/pmax | solution.py:27
  17.7 0.2 fusion.25
  17.9 4.9 %psum.28 = f32[4,32]{1,0:T(4,128)S(1)} all-reduce(f32[4,32]{1,0:T(4,128)S(1)} %fusion.25), channel_id=1, replica_groups=mesh['dp'=16,'tensor'=2] {'tensor'}, use_global_device_ids=true, to_apply=%region_3.0 | all-reduce | flops 128 | bytes 1024 | tf_op jit(solution)/shard_map/psum | solution.py:29
  22.9 1.1 fusion.29
  24.0 5.4 %reduce-scatter.5.cloned.1.call-done = f32[4,32,512]{2,1,0:T(8,128)} async-done(((f32[4,32,1024]{2,1,0:T(8,128)}), f32[4,32,512]{2,1,0:T(8,128)}) %reduce-scatter.5.cloned.1.call-update) | async-done | bytes 262160 | tf_op jit(solution)/shard_map/reduce_scatter | solution.py:8
  29.4 1.0 convert_element_type.38
  30.3 0.8 copy.13
  31.1 5.6 %all-to-all-start = ((bf16[4,32,512]{2,0,1:T(4,128)(2,1)}), bf16[4,32,512]{2,0,1:T(4,128)(2,1)S(1)}, u32[]{:S(2)}, u32[]{:S(2)}) async-start(bf16[4,32,512]{2,0,1:T(4,128)(2,1)} %copy.13), calls=%async_computation.1 | async-start | bytes 262144 | tf_op jit(solution)/shard_map/all_to_all | solution.py:11
  36.7 10.1 %reduce-scatter.7.cloned.1.call-done = f32[4,32,512]{2,1,0:T(8,128)} async-done(((f32[4,32,1024]{2,1,0:T(8,128)}), f32[4,32,512]{2,1,0:T(8,128)}) %reduce-scatter.7.cloned.1.call-update) | async-done | bytes 262160 | tf_op jit(solution)/shard_map/reduce_scatter | solution.py:8
  46.9 1.0 convert_element_type.39
  47.8 0.8 copy.15
  48.6 5.6 %all-to-all-start.1 = ((bf16[4,32,512]{2,0,1:T(4,128)(2,1)}), bf16[4,32,512]{2,0,1:T(4,128)(2,1)S(1)}, u32[]{:S(2)}, u32[]{:S(2)}) async-start(bf16[4,32,512]{2,0,1:T(4,128)(2,1)} %copy.15), calls=%async_computation.3 | async-start | bytes 262144 | tf_op jit(solution)/shard_map/all_to_all | solution.py:11
  54.4 6.5 %all_gather.12 = bf16[64,2,1024]{2,0,1:T(8,128)(2,1)S(1)} all-gather(bf16[64,2,512]{2,0,1:T(8,128)(2,1)S(1)} %all_to_all.55), channel_id=1, replica_groups=mesh['dp'=16,'tensor'=2] {'tensor'}, dimensions={2}, use_global_device_ids=true | all-gather | bytes 393216 | tf_op jit(solution)/shard_map/all_gather | solution.py:12
  60.8 1.3 all-to-all-done.1
  62.2 5.8 %all_gather.13 = bf16[64,2,1024]{2,0,1:T(8,128)(2,1)S(1)} all-gather(bf16[64,2,512]{2,0,1:T(8,128)(2,1)S(1)} %all_to_all.59), channel_id=1, replica_groups=mesh['dp'=16,'tensor'=2] {'tensor'}, dimensions={2}, use_global_device_ids=true | all-gather | bytes 393216 | tf_op jit(solution)/shard_map/all_gather | solution.py:12
  68.0 5.1 %convolution_bitcast_fusion = f32[64,2,2048]{2,0,1:T(8,128)S(1)} fusion(bf16[64,2,1024]{2,0,1:T(8,128)(2,1)S(1)} %all_gather.13, bf16[2,1024,2048]{2,1,0:T(8,128)(2,1)} %param.8), kind=kOutput, calls=%fused_computation.4 | convolution fusion | flops 536870912 | bytes 9699328 | tf_op jit(solution)/shard_map/ied,edf->ief/dot_general | solution.py:43
  73.1 2.9 %fusion.16 = bf16[64,2,2048]{2,0,1:T(8,128)(2,1)S(1)} fusion(f32[64,2,2048]{2,0,1:T(8,128)S(1)} %convolution_bitcast_fusion, bf16[64,2,1024]{2,0,1:T(8,128)(2,1)S(1)} %all_gather.12, bf16[2,2048,1024]{2,1,0:T(8,128)(2,1)S(1)} %copy-done.1), kind=kOutput, calls=%fused_computation.28 | convolution fusion | flops 542113792 | bytes 10223616 | tf_op jit(solution)/shard_map/ied,efd->ief/dot_general | solution.py:53
  76.0 3.5 %convolution_bitcast_fusion.3 = f32[64,2,1024]{2,0,1:T(8,128)} fusion(bf16[64,2,2048]{2,0,1:T(8,128)(2,1)S(1)} %fusion.16, bf16[2,1024,2048]{2,1,0:T(8,128)(2,1)S(1)} %bitcast.67), kind=kOutput, calls=%fused_computation.11 | convolution fusion | flops 536870912 | bytes 9437184 | tf_op jit(solution)/shard_map/ief,edf->ied/dot_general | solution.py:62
  79.6 5.7 %convolution_bitcast_fusion.2 = f32[64,2,1024]{2,0,1:T(8,128)} fusion(bf16[2,2048,1024]{2,1,0:T(8,128)(2,1)} %param.9, f32[64,2,2048]{2,0,1:T(8,128)S(1)} %convolution_bitcast_fusion), kind=kOutput, calls=%fused_computation.10 | convolution fusion | flops 539230208 | bytes 9961472 | tf_op jit(solution)/shard_map/ief,efd->ied/dot_general | solution.py:47
  85.3 5.8 %convolution_convert_fusion = bf16[2,2048,1024]{2,1,0:T(8,128)(2,1)} fusion(bf16[64,2,1024]{2,0,1:T(8,128)(2,1)S(1)} %all_gather.12, f32[64,2,2048]{2,0,1:T(8,128)S(1)} %convolution_bitcast_fusion), kind=kOutput, calls=%fused_computation.2 | convolution fusion | flops 543424512 | bytes 9699328 | tf_op jit(solution)/shard_map/ief,ied->efd/dot_general | solution.py:55
  91.1 2.0 reduce-scatter.9.cloned.1.call-done
  93.1 1.0 convert_element_type.41
  94.1 0.8 copy.17
  94.9 5.6 %all-to-all-start.2 = ((bf16[64,2,512]{2,1,0:T(2,128)(2,1)}), bf16[64,2,512]{2,1,0:T(2,128)(2,1)S(1)}, u32[]{:S(2)}, u32[]{:S(2)}) async-start(bf16[64,2,512]{2,1,0:T(2,128)(2,1)} %copy.17), calls=%async_computation.5 | async-start | bytes 262144 | tf_op jit(solution)/shard_map/all_to_all | solution.py:20
  100.5 5.8 %convolution_convert_fusion.1 = bf16[2,1024,2048]{2,1,0:T(8,128)(2,1)} fusion(bf16[64,2,1024]{2,0,1:T(8,128)(2,1)S(1)} %all_gather.13, bf16[64,2,2048]{2,0,1:T(8,128)(2,1)S(1)} %fusion.16), kind=kOutput, calls=%fused_computation.3 | convolution fusion | flops 541065216 | bytes 9175040 | tf_op jit(solution)/shard_map/ied,ief->edf/dot_general | solution.py:58
  106.3 4.2 %reduce-scatter.11.cloned.1.call-done = f32[64,2,512]{2,0,1:T(8,128)} async-done(((f32[64,2,1024]{2,0,1:T(8,128)}), f32[64,2,512]{2,0,1:T(8,128)}) %reduce-scatter.11.cloned.1.call-update) | async-done | bytes 262160 | tf_op jit(solution)/shard_map/reduce_scatter | solution.py:17
  110.4 1.0 convert_element_type.43
  111.4 0.8 copy.19
  112.2 5.6 %all-to-all-start.3 = ((bf16[64,2,512]{2,1,0:T(2,128)(2,1)}), bf16[64,2,512]{2,1,0:T(2,128)(2,1)S(1)}, u32[]{:S(2)}, u32[]{:S(2)}) async-start(bf16[64,2,512]{2,1,0:T(2,128)(2,1)} %copy.19), calls=%async_computation.7 | async-start | bytes 262144 | tf_op jit(solution)/shard_map/all_to_all | solution.py:20
  117.9 0.1 copy.26
  118.0 0.1 all_to_all.63
  118.1 6.5 %all_gather.14 = bf16[4,32,1024]{2,1,0:T(8,128)(2,1)S(1)} all-gather(bf16[4,32,512]{2,1,0:T(8,128)(2,1)S(1)} %all_to_all.63), channel_id=1, replica_groups=mesh['dp'=16,'tensor'=2] {'tensor'}, dimensions={2}, use_global_device_ids=true | all-gather | bytes 393216 | tf_op jit(solution)/shard_map/all_gather | solution.py:21
  124.5 0.4 multiply_reduce_fusion.1
  124.9 4.9 %psum.29 = f32[4,32]{1,0:T(4,128)S(1)} all-reduce(f32[4,32]{1,0:T(4,128)S(1)} %get-tuple-element.8), channel_id=1, replica_groups=mesh['dp'=16,'tensor'=2] {'tensor'}, use_global_device_ids=true, to_apply=%region_12.0 | all-reduce | flops 128 | bytes 1024 | tf_op jit(solution)/shard_map/psum | solution.py:65
  129.9 0.1 copy.25
  129.9 0.1 all_to_all.67
  130.0 5.6 %all_gather.15 = bf16[4,32,1024]{2,1,0:T(8,128)(2,1)S(1)} all-gather(bf16[4,32,512]{2,1,0:T(8,128)(2,1)S(1)} %all_to_all.67), channel_id=1, replica_groups=mesh['dp'=16,'tensor'=2] {'tensor'}, dimensions={2}, use_global_device_ids=true | all-gather | bytes 393216 | tf_op jit(solution)/shard_map/all_gather | solution.py:21
  135.7 0.3 convolution_bitcast_fusion.6
  135.9 1.0 convolution_bitcast_fusion.4
  137.1 0.4 fusion.9
  137.5 21.3 %all-reduce.3.cloned.1.call-done = f32[1024,32]{0,1:T(8,128)} async-done(((f32[1024,32]{0,1:T(8,128)}), f32[1024,32]{0,1:T(8,128)}) %all-reduce.3.cloned.1.call-update) | async-done | bytes 131088 | tf_op jit(solution)/shard_map/psum | solution.py:78
  158.8 1.3 fusion.2
  160.1 90.3 %all-reduce.5.cloned.1.call-done = f32[1024,32]{0,1:T(8,128)} async-done(((f32[1024,32]{0,1:T(8,128)}), f32[1024,32]{0,1:T(8,128)}) %all-reduce.5.cloned.1.call-update) | async-done | bytes 131088 | tf_op jit(solution)/shard_map/psum | solution.py:79
  250.4 1.6 copy.31
  (31 shorter events, 0.6 us)
Async XLA Ops:
  7.2 1.1 copy-start
  7.2 22.2 %reduce-scatter.5.cloned.1.call-start = ((), (), s32[]{:S(2)}) async-start(), calls=%async_computation.8 | async-start | bytes 786432 | tf_op jit(solution)/shard_map/reduce_scatter | solution.py:8
  11.8 35.0 %reduce-scatter.7.cloned.1.call-start = ((), (), s32[]{:S(2)}) async-start(), calls=%async_computation.9 | async-start | bytes 786432 | tf_op jit(solution)/shard_map/reduce_scatter | solution.py:8
  31.1 17.5 %all-to-all-start = ((bf16[4,32,512]{2,0,1:T(4,128)(2,1)}), bf16[4,32,512]{2,0,1:T(4,128)(2,1)S(1)}, u32[]{:S(2)}, u32[]{:S(2)}) async-start(bf16[4,32,512]{2,0,1:T(4,128)(2,1)} %copy.13), calls=%async_computation.1 | async-start | bytes 262144 | tf_op jit(solution)/shard_map/all_to_all | solution.py:11
  48.6 13.5 %all-to-all-start.1 = ((bf16[4,32,512]{2,0,1:T(4,128)(2,1)}), bf16[4,32,512]{2,0,1:T(4,128)(2,1)S(1)}, u32[]{:S(2)}, u32[]{:S(2)}) async-start(bf16[4,32,512]{2,0,1:T(4,128)(2,1)} %copy.15), calls=%async_computation.3 | async-start | bytes 262144 | tf_op jit(solution)/shard_map/all_to_all | solution.py:11
  54.2 38.9 %reduce-scatter.9.cloned.1.call-start = ((), (), s32[]{:S(2)}) async-start(), calls=%async_computation.10 | async-start | bytes 786432 | tf_op jit(solution)/shard_map/reduce_scatter | solution.py:17
  62.2 10.9 %copy-start.1 = (bf16[2,2048,1024]{2,1,0:T(8,128)(2,1)S(1)}, bf16[2,2048,1024]{2,1,0:T(8,128)(2,1)}, u32[]{:S(2)}) copy-start(bf16[2,2048,1024]{2,1,0:T(8,128)(2,1)} %param.9) | copy-start | bytes 25165828
  62.2 13.8 %slice-start = ((s8[8388608]{0:T(1024)(128)(4,1)}), s8[4194304]{0:T(1024)(128)(4,1)S(1)}, s32[]{:S(2)}) async-start(s8[8388608]{0:T(1024)(128)(4,1)} %bitcast.66), calls=%async_computation.14 | async-start | bytes 8388608
  68.0 8.0 %slice-start.1 = ((s8[8388608]{0:T(1024)(128)(4,1)}), s8[4194304]{0:T(1024)(128)(4,1)S(1)}, s32[]{:S(2)}) async-start(s8[8388608]{0:T(1024)(128)(4,1)} %bitcast.66), calls=%async_computation.15 | async-start | bytes 8388608
  79.5 30.9 %reduce-scatter.11.cloned.1.call-start = ((), (), s32[]{:S(2)}) async-start(), calls=%async_computation.11 | async-start | bytes 786432 | tf_op jit(solution)/shard_map/reduce_scatter | solution.py:17
  91.1 44.6 %copy-start.2 = (bf16[4,72,1024]{2,1,0:T(8,128)(2,1)S(1)}, bf16[4,72,1024]{2,1,0:T(8,128)(2,1)}, u32[]{:S(2)}) copy-start(bf16[4,72,1024]{2,1,0:T(8,128)(2,1)} %param.6) | copy-start | bytes 1769476
  91.1 46.0 %copy-start.3 = (bf16[1024,32]{0,1:T(8,128)(2,1)S(1)}, bf16[1024,32]{0,1:T(8,128)(2,1)}, u32[]{:S(2)}) copy-start(bf16[1024,32]{0,1:T(8,128)(2,1)} %param.7) | copy-start | bytes 196612
  94.9 17.3 %all-to-all-start.2 = ((bf16[64,2,512]{2,1,0:T(2,128)(2,1)}), bf16[64,2,512]{2,1,0:T(2,128)(2,1)S(1)}, u32[]{:S(2)}, u32[]{:S(2)}) async-start(bf16[64,2,512]{2,1,0:T(2,128)(2,1)} %copy.17), calls=%async_computation.5 | async-start | bytes 262144 | tf_op jit(solution)/shard_map/all_to_all | solution.py:20
  112.2 17.6 %all-to-all-start.3 = ((bf16[64,2,512]{2,1,0:T(2,128)(2,1)}), bf16[64,2,512]{2,1,0:T(2,128)(2,1)S(1)}, u32[]{:S(2)}, u32[]{:S(2)}) async-start(bf16[64,2,512]{2,1,0:T(2,128)(2,1)} %copy.19), calls=%async_computation.7 | async-start | bytes 262144 | tf_op jit(solution)/shard_map/all_to_all | solution.py:20
  117.9 40.9 %all-reduce.3.cloned.1.call-start = ((), (), s32[]{:S(2)}) async-start(), calls=%async_computation.12 | async-start | bytes 262144 | tf_op jit(solution)/shard_map/psum | solution.py:78
  137.0 113.3 %all-reduce.5.cloned.1.call-start = ((), (), s32[]{:S(2)}) async-start(), calls=%async_computation.13 | async-start | bytes 262144 | tf_op jit(solution)/shard_map/psum | solution.py:79
Sparse Core Ops, SparseCore 0:
  11.9 17.3 reduce-scatter.4
  32.2 14.6 reduce-scatter.6
  79.6 13.4 reduce-scatter.8
  95.8 14.6 reduce-scatter.10
  137.1 21.6 all-reduce.2
  162.1 88.2 all-reduce.4
